TPU v7x, 32 devices: a whole 2x2x4 slice. The times are simulated.
32 devices in a mesh: groups: 2 (over y), feat: 4 (over x, core), loop: 4 (over z).
Axes of the slice: x: 2, y: 2, z: 4, core: 2. Of those that a mesh axis runs over, the one named last changes fastest.
Arguments:
- train_grads: bfloat16 [512, 65536], P(('groups', 'loop'), 'feat'), parts along dimension 0, may hold values from -6 to 6
- query_grads: bfloat16 [64, 65536], P(('groups', 'loop'), 'feat'), parts along dimension 0, may hold values from -0.0234375 to 0.0234375
- curvature: float32 [65536], P('feat'), may hold values from 0.05 to 5
- row_counts: int32 [8], P(('groups', 'loop')), parts along dimension 0, may hold values from 1 to 64, 128 in all
Outputs:
- scores: float32 [512, 32], P(('groups', 'loop', 'feat')), parts along dimension 0
There are 2 independent parts, one for each index of `groups`. A program takes and returns all parts, laid end to end along the dimension named above; an argument that names none is the same for every part. Nothing has to cross between parts.
Inputs may be any that keep to these rules, and one draw needn't show every extreme that they name: row_counts[s] is the number of live slots of loop shard s; slots 0 to row_counts[s] - 1 of that shard are live; some shard has exactly 64; the counts sum to 128.
All inputs are finite; a program needn't handle non-finite values.
Results may differ from a plain program's by a relative error of at most 0.0029.
Values may be sent and summed in bfloat16 or wider, within the bound.
A program may use at most 128 MiB of HBM per device.

v0:
```python
import functools
import math

import jax
import jax.numpy as jnp
from jax import lax
from jax.experimental import pallas as pl
from jax.experimental.pallas import tpu as pltpu
from jax.sharding import PartitionSpec as P

MESH = pl.DeviceIdType.MESH
damping_term = 0.1


def kernel(
    n, nf, pieces, tail,
    t_hbm, q_hbm, c_hbm, count_hbm, out_ref,
    gath, t_ref, count_ref, c_ref, inv_ref, acc, part, red, t_tail, p_tail, tail_acc, tail_part, tail_red,
    local_sem, recv_sem, send_sem, red_recv, red_send, give_sem, tail_recv, tail_send, ready_sem,
):
    me, f = lax.axis_index("loop"), lax.axis_index("feat")
    rows, width = t_ref.shape
    own_rows = rows // nf
    q_rows = gath.shape[1]
    main = width - tail
    cols = main // pieces
    stride = pieces + 1
    has_left, has_right = me > 0, me < n - 1
    is_end = (me == 0) | (me == n - 1)
    is_helper = (me == 1) | (me == n - 2)

    load_q = pltpu.make_async_copy(q_hbm, gath.at[me], local_sem.at[0])
    load_c = pltpu.make_async_copy(c_hbm, c_ref, local_sem.at[1])
    load_t = pltpu.make_async_copy(t_hbm, t_ref, local_sem.at[2])
    load_count = pltpu.make_async_copy(count_hbm, count_ref, local_sem.at[3])
    load_q.start()

    barrier = pltpu.get_barrier_semaphore()

    @pl.when(has_right)
    def _():
        pl.semaphore_signal(barrier, inc=1, device_id={"loop": me + 1}, device_id_type=MESH)

    for k in range(1, nf):
        pl.semaphore_signal(
            barrier, inc=1, device_id={"feat": lax.rem(f + k, nf)}, device_id_type=MESH
        )
    load_c.start()
    load_t.start()
    load_count.start()

    def columns(piece):
        if piece is None:
            return pl.ds(main, tail)
        return pl.ds(pl.multiple_of(piece * cols, 128), cols)

    def hop(way, block, piece):
        span = gath.at[block, :, columns(piece)]
        at = block * stride + (pieces if piece is None else piece)
        return pltpu.make_async_remote_copy(
            src_ref=span,
            dst_ref=span,
            send_sem=send_sem.at[way, at],
            recv_sem=recv_sem.at[at],
            device_id={"loop": jnp.clip(me + (2 * way - 1), 0, n - 1)},
            device_id_type=MESH,
        )

    def goes_right(piece):
        return has_right if piece is not None else me < n - 2

    def goes_left(piece):
        return has_left if piece is not None else me > 1

    def multiply(block, piece):
        start, size = (main, tail) if piece is None else (piece * cols, cols)
        here = pl.ds(pl.multiple_of(block * q_rows, q_rows), q_rows)
        wide = size // 2 if size % 256 == 0 else size

        @pl.loop(0, size // wide)
        def _(step):
            at = pl.ds(pl.multiple_of(start + step * wide, 128), wide)
            exact = gath[block, :, at].astype(jnp.float32) * inv_ref[:, at]
            acc[here, 0:rows] += lax.dot_general(
                exact.astype(jnp.bfloat16), t_ref[:, at], (((1,), (1,)), ((), ())),
                preferred_element_type=jnp.float32,
            )
            if piece is None:
                p_tail[here, pl.ds(pl.multiple_of(step * wide, 128), wide)] = exact

    def arrive(back, piece):
        from_left, from_right = me - back, me + back
        takes_left, takes_right = from_left >= 0, from_right < n
        if piece is None:
            inner = jnp.logical_not(is_end)
            takes_left, takes_right = takes_left & inner, takes_right & inner
        moved = back > 0

        @pl.when(takes_left & moved)
        def _():
            hop(1, from_left, piece).wait_recv()

            @pl.when(goes_right(piece))
            def _():
                hop(1, from_left, piece).start()

        @pl.when(takes_right & moved)
        def _():
            hop(0, from_right, piece).wait_recv()

            @pl.when(goes_left(piece))
            def _():
                hop(0, from_right, piece).start()

        @pl.loop(0, 2)
        def _(side):
            @pl.when(((side == 0) & takes_left) | ((side == 1) & takes_right & moved))
            def _():
                multiply(me + (2 * side - 1) * back, piece)

    give = pltpu.make_async_remote_copy(
        src_ref=t_ref.at[:, pl.ds(main, t_tail.shape[1])],
        dst_ref=t_tail,
        send_sem=give_sem.at[0],
        recv_sem=give_sem.at[1],
        device_id={"loop": jnp.where(me == 0, 1, n - 2)},
        device_id_type=MESH,
    ) if tail else None

    acc[...] = jnp.zeros_like(acc)
    load_q.wait()
    pl.semaphore_wait(barrier, has_left.astype(jnp.int32) + nf - 1)

    @pl.when(has_left)
    def _():
        pl.semaphore_signal(ready_sem, inc=1, device_id={"loop": me - 1}, device_id_type=MESH)

        @pl.loop(0, pieces)
        def _(piece):
            hop(0, me, piece).start()

    if tail:
        @pl.when(goes_left(None))
        def _():
            hop(0, me, None).start()

    @pl.when(has_right)
    def _():
        pl.semaphore_wait(ready_sem, 1)

        @pl.loop(0, pieces)
        def _(piece):
            hop(1, me, piece).start()

    if tail:
        @pl.when(goes_right(None))
        def _():
            hop(1, me, None).start()

    load_t.wait()
    if tail:
        @pl.when(is_end)
        def _():
            give.start()

    load_c.wait()
    inv_ref[...] = 1.0 / (damping_term + c_ref[...])

    @pl.loop(0, n)
    def _(back):
        @pl.loop(0, pieces)
        def _(piece):
            arrive(back, piece)

        if tail:
            arrive(back, None)

    turned = acc[...].T
    for k in range(nf):
        part[k] = turned[k * own_rows:(k + 1) * own_rows, 0:part.shape[2]]

    shares = []
    for k in range(1, nf):
        peer = lax.rem(f + k, nf)
        share = pltpu.make_async_remote_copy(
            src_ref=part.at[peer],
            dst_ref=red.at[k - 1],
            send_sem=red_send.at[k - 1],
            recv_sem=red_recv.at[k - 1],
            device_id={"feat": peer},
            device_id_type=MESH,
        )
        share.start()
        shares.append(share)

    tail_shares = []
    if tail:
        for k in range(nf):
            peer = lax.rem(f + k, nf)
            tail_shares.append(pltpu.make_async_remote_copy(
                src_ref=tail_part.at[peer],
                dst_ref=tail_red.at[k],
                send_sem=tail_send.at[k],
                recv_sem=tail_recv.at[k],
                device_id={"feat": peer, "loop": jnp.where(me == 1, 0, n - 1)},
                device_id_type=MESH,
            ))

        @pl.when(is_helper)
        def _():
            give.wait_recv()
            tail_acc[...] = jnp.zeros_like(tail_acc)
            wide = math.gcd(tail, 512)

            @pl.loop(0, tail // wide)
            def _(step):
                at = pl.ds(pl.multiple_of(step * wide, 128), wide)
                tail_acc[...] += lax.dot_general(
                    t_tail[:, at], p_tail[:, at].astype(jnp.bfloat16), (((1,), (1,)), ((), ())),
                    preferred_element_type=jnp.float32,
                )

            for k in range(nf):
                tail_part[k] = tail_acc[k * own_rows:(k + 1) * own_rows, :]
            for share in tail_shares:
                share.start()

    @pl.loop(0, n)
    def _(block):
        def sent(piece):
            @pl.when(goes_right(piece) & (block <= me))
            def _():
                hop(1, block, piece).wait_send()

            @pl.when(goes_left(piece) & (block >= me))
            def _():
                hop(0, block, piece).wait_send()

        @pl.loop(0, pieces)
        def _(piece):
            sent(piece)

        if tail:
            sent(None)

    load_count.wait()
    live = f * own_rows + lax.broadcasted_iota(jnp.int32, out_ref.shape, 0) < count_ref[0]
    total = part[f]
    for k in range(1, nf):
        shares[k - 1].wait_recv()
        total = total + red[k - 1]
    out_ref[...] = jnp.where(live, total, 0.0)
    if tail:
        @pl.when(is_end)
        def _():
            more = jnp.zeros_like(total)
            for k in range(nf):
                tail_shares[k].wait_recv()
                more = more + tail_red[k]
            out_ref[...] = jnp.where(live, total + more, 0.0)
            give.wait_send()

        @pl.when(is_helper)
        def _():
            for share in tail_shares:
                share.wait_send()
    for share in shares:
        share.wait_send()


def on_device(n, nf, train_grads, query_grads, curvature, row_counts):
    rows, width = train_grads.shape
    q_rows = query_grads.shape[0]
    queries = n * q_rows
    pieces = max(1, 16 // n)
    unit = 128 * pieces
    tail = width - width * 27 // 32 // unit * unit if n >= 4 else 0
    padded = -(-queries // 128) * 128
    lanes = -(-rows // 128) * 128
    hbm = pl.BlockSpec(memory_space=pltpu.HBM)
    return pl.pallas_call(
        functools.partial(kernel, n, nf, pieces, tail),
        out_shape=pltpu.VMEM((rows // nf, queries), jnp.float32),
        in_specs=[hbm] * 4,
        out_specs=pl.BlockSpec(memory_space=pltpu.VMEM),
        scratch_shapes=[
            pltpu.VMEM((n, q_rows, width), jnp.bfloat16),
            pltpu.VMEM((rows, width), jnp.bfloat16),
            pltpu.SMEM((1,), jnp.int32),
            pltpu.VMEM((1, width), jnp.float32),
            pltpu.VMEM((1, width), jnp.float32),
            pltpu.VMEM((padded, lanes), jnp.float32),
            pltpu.VMEM((nf, rows // nf, queries), jnp.float32),
            pltpu.VMEM((nf - 1, rows // nf, queries), jnp.float32),
            pltpu.VMEM((rows, tail or 128), jnp.bfloat16),
            pltpu.VMEM((queries, tail or 128), jnp.float32),
            pltpu.VMEM((rows, queries), jnp.float32),
            pltpu.VMEM((nf, rows // nf, queries), jnp.float32),
            pltpu.VMEM((nf, rows // nf, queries), jnp.float32),
            pltpu.SemaphoreType.DMA((4,)),
            pltpu.SemaphoreType.DMA((n * (pieces + 1),)),
            pltpu.SemaphoreType.DMA((2, n * (pieces + 1))),
            pltpu.SemaphoreType.DMA((nf - 1,)),
            pltpu.SemaphoreType.DMA((nf - 1,)),
            pltpu.SemaphoreType.DMA((2,)),
            pltpu.SemaphoreType.DMA((nf,)),
            pltpu.SemaphoreType.DMA((nf,)),
            pltpu.SemaphoreType.REGULAR,
        ],
        compiler_params=pltpu.CompilerParams(collective_id=0, has_side_effects=True),
    )(train_grads, query_grads, curvature.reshape(1, width), row_counts)


def solution(mesh):
    placed = (
        P(("groups", "loop"), "feat"),
        P(("groups", "loop"), "feat"),
        P("feat"),
        P(("groups", "loop")),
    )
    return jax.shard_map(
        functools.partial(on_device, mesh.shape["loop"], mesh.shape["feat"]),
        mesh=mesh,
        in_specs=placed,
        out_specs=P(("groups", "loop", "feat"), None),
        check_vma=False,
    )
```

profile of v0, /device:TPU:0, one launch (start us, length us, event | category | flops | bytes accessed | tf_op | source)
XLA Modules:
  0.0 24.8 jit_solution(17021526526071282909)
XLA Ops:
  0.7 23.5 %shard_map.46 = f32[16,32]{1,0:T(8,128)S(1)} custom-call(bf16[64,16384]{1,0:T(8,128)(2,1)} %t_hbm.1, bf16[8,16384]{1,0:T(8,128)(2,1)} %q_hbm.1, f32[1,16384]{1,0:T(1,128)} %bitcast.1, s32[1]{0:T(128)S(6)} %copy.7.count_hbm), custom_call_target="tpu_custom_call" | custom-call | tf_op jit(solution)/shard_map/pallas_call | solution.py:281
  24.2 0.6 %copy.6 = f32[16,32]{1,0:T(8,128)} copy(f32[16,32]{1,0:T(8,128)S(1)} %shard_map.46) | data formatting | bytes 4096
where the time goes:
time: 24.9 us; the launch traced here: 24.8 us
  Pallas kernels  23.5 us (94%)
  between operations  0.66 us (3%)
  local copies, waits for them, and re-layouts  0.6 us (2%)
    pallas_call x1, Pallas kernels, on_device(): pl.pallas_call(functools.partial(kernel, n, nf, pieces, tail), out_shape=...  23.5 us
    unnamed x1, local copies, waits for them, and re-layouts  0.6 us

commit v1 on v0

v1 whole, which is shorter than its diff:
```python
import functools

import jax
import jax.numpy as jnp
from jax import lax
from jax.experimental import pallas as pl
from jax.experimental.pallas import tpu as pltpu
from jax.sharding import PartitionSpec as P

MESH = pl.DeviceIdType.MESH
damping_term = 0.1


def kernel(
    n, nf, cuts, split,
    t_hbm, q_hbm, c_hbm, count_ref, out_ref,
    gath, t_ref, c_ref, inv_ref, acc, part, red, t_tail, p_tail, tail_acc, tail_part,
    local_sem, recv_sem, share_sem, give_sem, ready_sem,
):
    me, f = lax.axis_index("loop"), lax.axis_index("feat")
    rows, width = t_ref.shape
    own_rows = rows // nf
    q_rows = gath.shape[1]
    pieces = len(cuts) - 1
    sizes = [cuts[p + 1] - cuts[p] for p in range(pieces)]
    mid, last = pieces - 2, pieces - 1
    has_left, has_right = me > 0, me < n - 1
    is_end = (me == 0) | (me == n - 1)
    is_helper = (me == 1) | (me == n - 2)
    even = lax.rem(f, 2) == 0

    def tail_here(piece):
        if not split or piece < mid:
            return False
        return True if piece == last else even

    load_q = [
        pltpu.make_async_copy(
            q_hbm.at[:, pl.ds(a, b - a)], gath.at[me, :, pl.ds(a, b - a)], local_sem.at[i]
        )
        for i, (a, b) in enumerate(((0, cuts[1]), (cuts[1], width)))
    ]
    load_c = pltpu.make_async_copy(c_hbm, c_ref, local_sem.at[3])
    load_t = pltpu.make_async_copy(t_hbm, t_ref, local_sem.at[2])
    for load in load_q:
        load.start()

    barrier = pltpu.get_barrier_semaphore()

    @pl.when(has_right)
    def _():
        pl.semaphore_signal(barrier, inc=1, device_id={"loop": me + 1}, device_id_type=MESH)

    for k in range(1, nf):
        pl.semaphore_signal(
            barrier, inc=1, device_id={"feat": lax.rem(f + k, nf)}, device_id_type=MESH
        )
    load_c.start()
    load_t.start()

    def columns(piece):
        return pl.ds(cuts[piece], sizes[piece])

    def hop(way, block, piece, taker):
        span = gath.at[block, :, columns(piece)]
        slot = block - (block > taker).astype(jnp.int32)
        return pltpu.make_async_remote_copy(
            src_ref=span,
            dst_ref=span,
            send_sem=local_sem.at[way],
            recv_sem=recv_sem.at[slot * pieces + piece],
            device_id={"loop": jnp.clip(me + (2 * way - 1), 0, n - 1)},
            device_id_type=MESH,
        )

    def goes(way, piece):
        there = has_right if way else has_left
        inner = me < n - 2 if way else me > 1
        tail = tail_here(piece)
        if tail is False:
            return there
        return inner if tail is True else there & (inner | jnp.logical_not(tail))

    def give(piece):
        at = pl.ds(cuts[piece] - cuts[mid], sizes[piece])
        return pltpu.make_async_remote_copy(
            src_ref=t_ref.at[:, columns(piece)],
            dst_ref=t_tail.at[:, at],
            send_sem=local_sem.at[3],
            recv_sem=give_sem.at[piece - mid],
            device_id={"loop": jnp.where(me == 0, 1, n - 2)},
            device_id_type=MESH,
        )

    def multiply(block, piece):
        here = pl.ds(pl.multiple_of(block * q_rows, q_rows), q_rows)
        exact = gath[block, :, columns(piece)].astype(jnp.float32) * inv_ref[:, columns(piece)]
        acc[here, 0:rows] += lax.dot_general(
            exact.astype(jnp.bfloat16), t_ref[:, columns(piece)], (((1,), (1,)), ((), ())),
            preferred_element_type=jnp.float32,
        )
        if split and piece >= mid:
            p_tail[here, pl.ds(cuts[piece] - cuts[mid], sizes[piece])] = exact

    mains = [(piece, True if tail_here(piece) is False else jnp.logical_not(even))
             for piece in range(pieces) if tail_here(piece) is not True]
    tails = [(piece, tail_here(piece)) for piece in range(pieces) if tail_here(piece) is not False]

    def take(way, block, piece):
        hop(way, block, piece, me).wait_recv()

        @pl.when(goes(way, piece))
        def _():
            hop(way, block, piece, me + 2 * way - 1).start()

    def arrive(back, piece, applies):
        from_left, from_right = me - back, me + back
        takes_left, takes_right = (from_left >= 0) & applies, (from_right < n) & applies
        moved = back > 0

        @pl.when(takes_right & moved)
        def _():
            take(0, from_right, piece)

        @pl.when(takes_left & moved)
        def _():
            take(1, from_left, piece)

        @pl.loop(0, 2)
        def _(side):
            @pl.when(((side == 0) & takes_left) | ((side == 1) & takes_right & moved))
            def _():
                multiply(me + (2 * side - 1) * back, piece)

    def own_mains(way):
        for piece, applies in mains:
            @pl.when(goes(way, piece) & applies)
            def _():
                hop(way, me, piece, me + 2 * way - 1).start()

    def own_tails(way):
        for piece, applies in tails:
            @pl.when(goes(way, piece) & applies)
            def _():
                hop(way, me, piece, me + 2 * way - 1).start()

    def arrive_tails(way, count):
        own_tails(way)

        @pl.loop(1, count + 1)
        def _(back):
            block = me + (1 - 2 * way) * back
            for piece, applies in tails:
                @pl.when(applies)
                def _():
                    take(way, block, piece)
                    multiply(block, piece)

    acc[...] = jnp.zeros_like(acc)
    pl.semaphore_wait(barrier, has_left.astype(jnp.int32) + nf - 1)

    @pl.when(has_left)
    def _():
        pl.semaphore_signal(ready_sem, inc=1, device_id={"loop": me - 1}, device_id_type=MESH)

    load_q[0].wait()

    @pl.when(has_left)
    def _():
        hop(0, me, 0, me - 1).start()

    load_q[1].wait()

    @pl.when(has_left)
    def _():
        for piece, applies in mains[1:]:
            @pl.when(goes(0, piece) & applies)
            def _():
                hop(0, me, piece, me - 1).start()

    if split:
        @pl.when(me == n - 1)
        def _():
            own_tails(0)

    @pl.when(has_right)
    def _():
        pl.semaphore_wait(ready_sem, 1)
        own_mains(1)

    if split:
        @pl.when(me == 0)
        def _():
            own_tails(1)

    load_c.wait()
    load_t.wait()
    if split:
        @pl.when(is_end & even)
        def _():
            give(mid).start()
            give(last).start()

    inv_ref[...] = 1.0 / (damping_term + c_ref[...])

    @pl.loop(0, n)
    def _(back):
        for piece, applies in mains:
            arrive(back, piece, applies)
            if split and piece == GIVE_PIECE:
                @pl.when(is_end & jnp.logical_not(even) & (back == n - GIVE_BACK))
                def _():
                    give(last).start()

        if split:
            @pl.when((back == 0) & jnp.logical_not(is_end))
            def _():
                for piece, applies in tails:
                    @pl.when(applies)
                    def _():
                        multiply(me, piece)

            for way in range(2):
                count = me if way else n - 1 - me

                @pl.when((back == count) & jnp.logical_not(is_end))
                def _():
                    arrive_tails(way, count)

    turned = acc[...].T
    for k in range(nf):
        part[k] = turned[k * own_rows:(k + 1) * own_rows, 0:part.shape[2]]

    def share(k):
        peer = lax.rem(f + k, nf)
        return pltpu.make_async_remote_copy(
            src_ref=part.at[peer],
            dst_ref=red.at[k - 1],
            send_sem=local_sem.at[2],
            recv_sem=share_sem.at[0],
            device_id={"feat": peer},
            device_id_type=MESH,
        )

    def tail_share(k):
        peer = lax.rem(f + k, nf)
        return pltpu.make_async_remote_copy(
            src_ref=tail_part.at[peer],
            dst_ref=red.at[nf - 1 + k],
            send_sem=local_sem.at[2],
            recv_sem=share_sem.at[0],
            device_id={"feat": peer, "loop": jnp.where(me == 1, 0, n - 1)},
            device_id_type=MESH,
        )

    for k in range(1, nf):
        share(k).start()

    def tail_dot(piece):
        at = pl.ds(cuts[piece] - cuts[mid], sizes[piece])
        return lax.dot_general(
            t_tail[:, at], p_tail[:, at].astype(jnp.bfloat16), (((1,), (1,)), ((), ())),
            preferred_element_type=jnp.float32,
        )

    def hand_over(total):
        for k in range(nf):
            tail_part[k] = total[k * own_rows:(k + 1) * own_rows, :]
        for k in range(nf):
            tail_share(k).start()

    if split:
        @pl.when(is_helper & even)
        def _():
            give(mid).wait_recv()
            tail_acc[...] = tail_dot(mid)
            give(last).wait_recv()
            hand_over(tail_acc[...] + tail_dot(last))

        @pl.when(is_helper & jnp.logical_not(even))
        def _():
            give(last).wait_recv()
            hand_over(tail_dot(last))

    def sent(way, blocks, wide):
        span = gath.at[pl.ds(0, blocks), :, pl.ds(0, wide)]
        pltpu.make_async_remote_copy(
            src_ref=span,
            dst_ref=span,
            send_sem=local_sem.at[way],
            recv_sem=recv_sem.at[0],
            device_id={"loop": jnp.clip(me + (2 * way - 1), 0, n - 1)},
            device_id_type=MESH,
        ).wait_send()

    for blocks in range(1, n):
        for way in range(2):
            at = me == (blocks - 1 if way else n - blocks)
            if not split or blocks < n - 1:
                @pl.when(at)
                def _():
                    sent(way, blocks, width)
            else:
                for wide, which in ((cuts[mid], even), (cuts[last], jnp.logical_not(even))):
                    @pl.when(at & which)
                    def _():
                        sent(way, blocks, wide)

    if split:
        for start, which in ((mid, even), (last, jnp.logical_not(even))):
            @pl.when(is_end & which)
            def _():
                span = pl.ds(cuts[start], width - cuts[start])
                pltpu.make_async_remote_copy(
                    src_ref=t_ref.at[:, span],
                    dst_ref=t_ref.at[:, span],
                    send_sem=local_sem.at[3],
                    recv_sem=give_sem.at[0],
                    device_id={"loop": jnp.where(me == 0, 1, n - 2)},
                    device_id_type=MESH,
                ).wait_send()

    def shares_in(count):
        pltpu.make_async_remote_copy(
            src_ref=red.at[pl.ds(0, count)],
            dst_ref=red.at[pl.ds(0, count)],
            send_sem=local_sem.at[2],
            recv_sem=share_sem.at[0],
            device_id={"feat": lax.rem(f + 1, nf)},
            device_id_type=MESH,
        ).wait_recv()

    def shares_out(count):
        pltpu.make_async_remote_copy(
            src_ref=red.at[pl.ds(0, count)],
            dst_ref=red.at[pl.ds(0, count)],
            send_sem=local_sem.at[2],
            recv_sem=share_sem.at[0],
            device_id={"feat": lax.rem(f + 1, nf)},
            device_id_type=MESH,
        ).wait_send()

    live = f * own_rows + lax.broadcasted_iota(jnp.int32, out_ref.shape, 0) < count_ref[0]

    def finish(count):
        shares_in(count)
        total = part[f]
        for k in range(count):
            total = total + red[k]
        out_ref[...] = jnp.where(live, total, 0.0)

    if split:
        @pl.when(is_end)
        def _():
            finish(2 * nf - 1)

        @pl.when(jnp.logical_not(is_end))
        def _():
            finish(nf - 1)

        @pl.when(is_helper)
        def _():
            shares_out(2 * nf - 1)

        @pl.when(jnp.logical_not(is_helper))
        def _():
            shares_out(nf - 1)
    else:
        finish(nf - 1)
        shares_out(nf - 1)


GIVE_PIECE = 2
GIVE_BACK = 2
EVEN_TAIL = 29
ODD_TAIL = 9


def on_device(n, nf, train_grads, query_grads, curvature, row_counts):
    rows, width = train_grads.shape
    q_rows = query_grads.shape[0]
    queries = n * q_rows
    split = n >= 4
    even_tail = width * EVEN_TAIL // 128 // 128 * 128
    odd_tail = width * ODD_TAIL // 128 // 128 * 128
    main = width - even_tail
    cuts = [main * i // 4 // 128 * 128 for i in range(4)] + [main, width - odd_tail, width]
    lanes = -(-rows // 128) * 128
    tail = width - main
    hbm = pl.BlockSpec(memory_space=pltpu.HBM)
    return pl.pallas_call(
        functools.partial(kernel, n, nf, cuts, split),
        out_shape=pltpu.VMEM((rows // nf, queries), jnp.float32),
        in_specs=[hbm] * 3 + [pl.BlockSpec(memory_space=pltpu.SMEM)],
        out_specs=pl.BlockSpec(memory_space=pltpu.VMEM),
        scratch_shapes=[
            pltpu.VMEM((n, q_rows, width), jnp.bfloat16),
            pltpu.VMEM((rows, width), jnp.bfloat16),
            pltpu.VMEM((1, width), jnp.float32),
            pltpu.VMEM((1, width), jnp.float32),
            pltpu.VMEM((queries, lanes), jnp.float32),
            pltpu.VMEM((nf, rows // nf, queries), jnp.float32),
            pltpu.VMEM((2 * nf - 1, rows // nf, queries), jnp.float32),
            pltpu.VMEM((rows, tail), jnp.bfloat16),
            pltpu.VMEM((queries, tail), jnp.float32),
            pltpu.VMEM((rows, queries), jnp.float32),
            pltpu.VMEM((nf, rows // nf, queries), jnp.float32),
            pltpu.SemaphoreType.DMA((4,)),
            pltpu.SemaphoreType.DMA(((n - 1) * (len(cuts) - 1),)),
            pltpu.SemaphoreType.DMA((1,)),
            pltpu.SemaphoreType.DMA((2,)),
            pltpu.SemaphoreType.REGULAR,
        ],
        compiler_params=pltpu.CompilerParams(collective_id=0, has_side_effects=True),
    )(train_grads, query_grads, curvature.reshape(1, width), row_counts)


def solution(mesh):
    placed = (
        P(("groups", "loop"), "feat"),
        P(("groups", "loop"), "feat"),
        P("feat"),
        P(("groups", "loop")),
    )
    return jax.shard_map(
        functools.partial(on_device, mesh.shape["loop"], mesh.shape["feat"]),
        mesh=mesh,
        in_specs=placed,
        out_specs=P(("groups", "loop", "feat"), None),
        check_vma=False,
    )
```

time: 24.9 us -> 23.6 us (0.948)
  Pallas kernels: 23.5 us -> 22.2 us
    pallas_call x1, Pallas kernels: 23.5 us -> 22.2 us  [on_device(): pl.pallas_call(functools.partial(kernel, n, nf, cuts, split), out_shape=p...]
where the time goes in v1:
time: 23.6 us; the launch traced here: 23.4 us
  Pallas kernels  22.2 us (94%)
  between operations  0.66 us (3%)
  local copies, waits for them, and re-layouts  0.6 us (3%)
    pallas_call x1, Pallas kernels, on_device(): pl.pallas_call(functools.partial(kernel, n, nf, cuts, split), out_shape=p...  22.2 us
    unnamed x1, local copies, waits for them, and re-layouts  0.6 us

profile of v1, /device:TPU:0, one launch (start us, length us, event | category | flops | bytes accessed | tf_op | source)
XLA Modules:
  0.0 23.4 jit_solution(6076365344729846275)
XLA Ops:
  0.7 22.2 %shard_map.46 = f32[16,32]{1,0:T(8,128)S(1)} custom-call(bf16[64,16384]{1,0:T(8,128)(2,1)} %t_hbm.1, bf16[8,16384]{1,0:T(8,128)(2,1)} %q_hbm.1, f32[1,16384]{1,0:T(1,128)} %bitcast.1, s32[1]{0:T(128)S(6)} %copy.7.count_ref), custom_call_target="tpu_custom_call" | custom-call | tf_op jit(solution)/shard_map/pallas_call | solution.py:391
  22.8 0.6 %copy.6 = f32[16,32]{1,0:T(8,128)} copy(f32[16,32]{1,0:T(8,128)S(1)} %shard_map.46) | data formatting | bytes 4096

commit v2 on v1

v2 whole, which is shorter than its diff:
```python
import functools

import jax
import jax.numpy as jnp
from jax import lax
from jax.experimental import pallas as pl
from jax.experimental.pallas import tpu as pltpu
from jax.sharding import PartitionSpec as P

MESH = pl.DeviceIdType.MESH
damping_term = 0.1
MAINS = ((21, 42, 63, 84, 96), (24, 48, 72, 96, 116))
GIVES = ((116, 128), (128,))
GIVE_AT = (None, (2, 3))
UNITS = 128


def kernel(
    n, nf, mains, gives, give_at,
    t_hbm, q_hbm, c_hbm, count_ref, out_ref,
    q_ref, gath, t_ref, c_ref, inv_ref, acc, part, red, t_tail, p_tail, tail_acc, tail_part,
    local_sem, recv_sem, share_sem, give_sem, ready_sem,
):
    me, f = lax.axis_index("loop"), lax.axis_index("feat")
    rows, width = t_ref.shape
    own_rows = rows // nf
    q_rows = q_ref.shape[0]
    slots = max(len(cuts) for cuts in mains)
    has_left, has_right = me > 0, me < n - 1
    is_first = me == 0
    is_end = is_first | (me == n - 1)
    is_helper = (me == 1) | (me == n - 2)
    head = max(cuts[1] for cuts in mains)

    load_q = [
        pltpu.make_async_copy(
            q_hbm.at[:, pl.ds(a, b - a)], q_ref.at[:, pl.ds(a, b - a)], local_sem.at[i]
        )
        for i, (a, b) in enumerate(((0, head), (head, width)))
    ]
    load_c = pltpu.make_async_copy(c_hbm, c_ref, local_sem.at[3])
    load_t = pltpu.make_async_copy(t_hbm, t_ref, local_sem.at[2])
    for load in load_q:
        load.start()

    barrier = pltpu.get_barrier_semaphore()

    @pl.when(has_right)
    def _():
        pl.semaphore_signal(barrier, inc=1, device_id={"loop": me + 1}, device_id_type=MESH)

    @pl.when(me == 1)
    def _():
        pl.semaphore_signal(barrier, inc=1, device_id={"loop": me - 1}, device_id_type=MESH)

    for k in range(1, nf):
        pl.semaphore_signal(
            barrier, inc=1, device_id={"feat": lax.rem(f + k, nf)}, device_id_type=MESH
        )
    load_c.start()
    load_t.start()
    acc[...] = jnp.zeros_like(acc)
    pl.semaphore_wait(barrier, jnp.where(is_first, has_right, has_left).astype(jnp.int32) + nf - 1)

    @pl.when(me > 1)
    def _():
        pl.semaphore_signal(ready_sem, inc=1, device_id={"loop": me - 1}, device_id_type=MESH)

    load_q[0].wait()

    def share(k):
        peer = lax.rem(f + k, nf)
        return pltpu.make_async_remote_copy(
            src_ref=part.at[peer],
            dst_ref=red.at[k - 1],
            send_sem=local_sem.at[2],
            recv_sem=share_sem.at[0],
            device_id={"feat": peer},
            device_id_type=MESH,
        )

    def tail_share(k):
        peer = lax.rem(f + k, nf)
        return pltpu.make_async_remote_copy(
            src_ref=tail_part.at[peer],
            dst_ref=red.at[nf - 1 + k],
            send_sem=local_sem.at[2],
            recv_sem=share_sem.at[0],
            device_id={"feat": peer, "loop": jnp.where(me == 1, 0, n - 1)},
            device_id_type=MESH,
        )

    def all_shares(count):
        return pltpu.make_async_remote_copy(
            src_ref=red.at[pl.ds(0, count)],
            dst_ref=red.at[pl.ds(0, count)],
            send_sem=local_sem.at[2],
            recv_sem=share_sem.at[0],
            device_id={"feat": lax.rem(f + 1, nf)},
            device_id_type=MESH,
        )

    def run(cuts, gift, give_when):
        count = len(cuts) - 1
        main = cuts[-1]
        tail = main < width

        def columns(piece):
            a = cuts[piece]
            b = cuts[piece + 1] if piece < count else width
            return pl.ds(a, b - a)

        def hop(way, block, piece, taker, own=False):
            span = gath.at[block, :, columns(piece)]
            slot = block - (block > taker).astype(jnp.int32)
            return pltpu.make_async_remote_copy(
                src_ref=q_ref.at[:, columns(piece)] if own else span,
                dst_ref=span,
                send_sem=local_sem.at[way],
                recv_sem=recv_sem.at[slot * slots + piece],
                device_id={"loop": jnp.clip(me + (2 * way - 1), 0, n - 1)},
                device_id_type=MESH,
            )

        def goes(way, piece):
            if piece < count:
                return has_right if way else has_left
            return me < n - 2 if way else me > 1

        def send_own(way, pieces):
            @pl.when(goes(way, pieces[0]))
            def _():
                for piece in pieces:
                    hop(way, me, piece, me + 2 * way - 1, own=True).start()

        def give(i):
            a, b = gift[i], gift[i + 1]
            return pltpu.make_async_remote_copy(
                src_ref=t_ref.at[:, pl.ds(a, b - a)],
                dst_ref=t_tail.at[:, pl.ds(a - main, b - a)],
                send_sem=local_sem.at[3],
                recv_sem=give_sem.at[i],
                device_id={"loop": jnp.where(is_first, 1, n - 2)},
                device_id_type=MESH,
            )

        def start_give():
            for i in range(len(gift) - 1):
                give(i).start()

        def multiply(block, piece, own=False):
            here = pl.ds(pl.multiple_of(block * q_rows, q_rows), q_rows)
            held = q_ref[:, columns(piece)] if own else gath[block, :, columns(piece)]
            exact = held.astype(jnp.float32) * inv_ref[:, columns(piece)]
            acc[here, 0:rows] += lax.dot_general(
                exact.astype(jnp.bfloat16), t_ref[:, columns(piece)], (((1,), (1,)), ((), ())),
                preferred_element_type=jnp.float32,
            )
            if piece == count:
                p_tail[here, 0:width - main] = exact

        def take(way, block, piece):
            hop(way, block, piece, me).wait_recv()

            @pl.when(goes(way, piece))
            def _():
                hop(way, block, piece, me + 2 * way - 1).start()

        def arrive(back, piece):
            from_left, from_right = me - back, me + back
            takes_left, takes_right = from_left >= 0, from_right < n

            @pl.when(takes_right)
            def _():
                take(0, from_right, piece)

            @pl.when(takes_left)
            def _():
                take(1, from_left, piece)

            @pl.loop(0, 2)
            def _(side):
                @pl.when(((side == 0) & takes_left) | ((side == 1) & takes_right))
                def _():
                    multiply(me + (2 * side - 1) * back, piece)

        send_own(0, [0])
        load_q[1].wait()
        send_own(0, range(1, count))
        if tail:
            @pl.when(me == n - 1)
            def _():
                send_own(0, [count])

        @pl.when(has_right & jnp.logical_not(is_first))
        def _():
            pl.semaphore_wait(ready_sem, 1)

        send_own(1, range(count))
        if tail:
            @pl.when(is_first)
            def _():
                send_own(1, [count])

        load_c.wait()
        load_t.wait()
        if tail and give_when is None:
            @pl.when(is_end)
            def _():
                start_give()

        inv_ref[...] = 1.0 / (damping_term + c_ref[...])
        for piece in range(count):
            multiply(me, piece, own=True)
        if tail:
            @pl.when(jnp.logical_not(is_end))
            def _():
                multiply(me, count, own=True)

        @pl.loop(1, n)
        def _(back):
            for piece in range(count):
                arrive(back, piece)
                if tail and give_when is not None and piece == give_when[1]:
                    @pl.when(is_end & (back == n - give_when[0]))
                    def _():
                        start_give()

            if tail:
                for way in range(2):
                    deep = me if way else n - 1 - me

                    @pl.when((back == deep) & jnp.logical_not(is_end))
                    def _():
                        send_own(way, [count])

                        @pl.loop(1, deep + 1)
                        def _(far):
                            block = me + (1 - 2 * way) * far
                            take(way, block, count)
                            multiply(block, count)

        turned = acc[...].T
        for k in range(nf):
            part[k] = turned[k * own_rows:(k + 1) * own_rows, 0:part.shape[2]]
        for k in range(1, nf):
            share(k).start()

        def tail_dot(i):
            at = pl.ds(gift[i] - main, gift[i + 1] - gift[i])
            return lax.dot_general(
                t_tail[:, at], p_tail[:, at].astype(jnp.bfloat16), (((1,), (1,)), ((), ())),
                preferred_element_type=jnp.float32,
            )

        if tail:
            @pl.when(is_helper)
            def _():
                total = None
                for i in range(len(gift) - 1):
                    give(i).wait_recv()
                    total = tail_dot(i) if total is None else tail_acc[...] + tail_dot(i)
                    if i < len(gift) - 2:
                        tail_acc[...] = total
                for k in range(nf):
                    tail_part[k] = total[k * own_rows:(k + 1) * own_rows, :]
                for k in range(nf):
                    tail_share(k).start()

        def sent(way, blocks, wide):
            span = gath.at[pl.ds(0, blocks), :, pl.ds(0, wide)]
            pltpu.make_async_remote_copy(
                src_ref=span,
                dst_ref=span,
                send_sem=local_sem.at[way],
                recv_sem=recv_sem.at[0],
                device_id={"loop": jnp.clip(me + (2 * way - 1), 0, n - 1)},
                device_id_type=MESH,
            ).wait_send()

        for blocks in range(1, n):
            for way in range(2):
                @pl.when(me == (blocks - 1 if way else n - blocks))
                def _():
                    sent(way, blocks, width if blocks < n - 1 else main)

        if tail:
            @pl.when(is_end)
            def _():
                span = t_ref.at[:, pl.ds(main, width - main)]
                pltpu.make_async_remote_copy(
                    src_ref=span,
                    dst_ref=span,
                    send_sem=local_sem.at[3],
                    recv_sem=give_sem.at[0],
                    device_id={"loop": jnp.where(is_first, 1, n - 2)},
                    device_id_type=MESH,
                ).wait_send()

    if mains[0] == mains[1]:
        run(mains[0], gives[0], give_at[0])
    else:
        for parity in range(2):
            @pl.when(lax.rem(f, 2) == parity)
            def _():
                run(mains[parity], gives[parity], give_at[parity])

    live = f * own_rows + lax.broadcasted_iota(jnp.int32, out_ref.shape, 0) < count_ref[0]

    def finish(count):
        all_shares(count).wait_recv()
        total = part[f]
        for k in range(count):
            total = total + red[k]
        out_ref[...] = jnp.where(live, total, 0.0)

    if mains[0][-1] == width:
        finish(nf - 1)
        all_shares(nf - 1).wait_send()
    else:
        @pl.when(is_end)
        def _():
            finish(2 * nf - 1)

        @pl.when(jnp.logical_not(is_end))
        def _():
            finish(nf - 1)

        @pl.when(is_helper)
        def _():
            all_shares(2 * nf - 1).wait_send()

        @pl.when(jnp.logical_not(is_helper))
        def _():
            all_shares(nf - 1).wait_send()


def on_device(n, nf, train_grads, query_grads, curvature, row_counts):
    rows, width = train_grads.shape
    q_rows = query_grads.shape[0]
    queries = n * q_rows

    def columns(cut):
        return width * cut // UNITS // 128 * 128

    if n >= 4:
        mains = [[0] + [columns(cut) for cut in cuts] for cuts in MAINS]
        gives = [
            [cuts[-1]] + [columns(cut) for cut in ends[:-1]] + [width]
            for cuts, ends in zip(mains, GIVES)
        ]
    else:
        mains = [[0] + [columns(cut) for cut in (32, 64, 96)] + [width]] * 2
        gives = [[width]] * 2
    tail = max(width - cuts[-1] for cuts in mains) or 128
    slots = max(len(cuts) for cuts in mains)
    lanes = -(-rows // 128) * 128
    hbm = pl.BlockSpec(memory_space=pltpu.HBM)
    return pl.pallas_call(
        functools.partial(kernel, n, nf, mains, gives, GIVE_AT),
        out_shape=pltpu.VMEM((rows // nf, queries), jnp.float32),
        in_specs=[hbm] * 3 + [pl.BlockSpec(memory_space=pltpu.SMEM)],
        out_specs=pl.BlockSpec(memory_space=pltpu.VMEM),
        scratch_shapes=[
            pltpu.VMEM((q_rows, width), jnp.bfloat16),
            pltpu.VMEM((n, q_rows, width), jnp.bfloat16),
            pltpu.VMEM((rows, width), jnp.bfloat16),
            pltpu.VMEM((1, width), jnp.float32),
            pltpu.VMEM((1, width), jnp.float32),
            pltpu.VMEM((queries, lanes), jnp.float32),
            pltpu.VMEM((nf, rows // nf, queries), jnp.float32),
            pltpu.VMEM((2 * nf - 1, rows // nf, queries), jnp.float32),
            pltpu.VMEM((rows, tail), jnp.bfloat16),
            pltpu.VMEM((queries, tail), jnp.float32),
            pltpu.VMEM((rows, queries), jnp.float32),
            pltpu.VMEM((nf, rows // nf, queries), jnp.float32),
            pltpu.SemaphoreType.DMA((4,)),
            pltpu.SemaphoreType.DMA(((n - 1) * slots,)),
            pltpu.SemaphoreType.DMA((1,)),
            pltpu.SemaphoreType.DMA((max(1, max(len(ends) - 1 for ends in gives)),)),
            pltpu.SemaphoreType.REGULAR,
        ],
        compiler_params=pltpu.CompilerParams(collective_id=0, has_side_effects=True),
    )(train_grads, query_grads, curvature.reshape(1, width), row_counts)


def solution(mesh):
    placed = (
        P(("groups", "loop"), "feat"),
        P(("groups", "loop"), "feat"),
        P("feat"),
        P(("groups", "loop")),
    )
    return jax.shard_map(
        functools.partial(on_device, mesh.shape["loop"], mesh.shape["feat"]),
        mesh=mesh,
        in_specs=placed,
        out_specs=P(("groups", "loop", "feat"), None),
        check_vma=False,
    )
```

time: 23.6 us -> 23.1 us (0.979)
  Pallas kernels: 22.2 us -> 21.7 us
    pallas_call x1, Pallas kernels: 22.2 us -> 21.7 us  [on_device(): pl.pallas_call(functools.partial(kernel, n, nf, mains, gives, GIVE_AT), o...]
where the time goes in v2:
time: 23.1 us; the launch traced here: 23 us
  Pallas kernels  21.7 us (94%)
  between operations  0.66 us (3%)
  local copies, waits for them, and re-layouts  0.6 us (3%)
    pallas_call x1, Pallas kernels, on_device(): pl.pallas_call(functools.partial(kernel, n, nf, mains, gives, GIVE_AT), o...  21.7 us
    unnamed x1, local copies, waits for them, and re-layouts  0.6 us

profile of v2, /device:TPU:0, one launch (start us, length us, event | category | flops | bytes accessed | tf_op | source)
XLA Modules:
  0.0 23.0 jit_solution(3828445694223703333)
XLA Ops:
  0.7 21.7 %shard_map.46 = f32[16,32]{1,0:T(8,128)S(1)} custom-call(bf16[64,16384]{1,0:T(8,128)(2,1)} %t_hbm.1, bf16[8,16384]{1,0:T(8,128)(2,1)} %q_hbm.1, f32[1,16384]{1,0:T(1,128)} %bitcast.1, s32[1]{0:T(128)S(6)} %copy.7.count_ref), custom_call_target="tpu_custom_call" | custom-call | tf_op jit(solution)/shard_map/pallas_call | solution.py:359
  22.4 0.6 %copy.6 = f32[16,32]{1,0:T(8,128)} copy(f32[16,32]{1,0:T(8,128)S(1)} %shard_map.46) | data formatting | bytes 4096

commit v3 on v2

--- a/solution.py
+++ b/solution.py
@@ -9,21 +9,24 @@
 
 MESH = pl.DeviceIdType.MESH
 damping_term = 0.1
-MAINS = ((21, 42, 63, 84, 96), (24, 48, 72, 96, 116))
-GIVES = ((116, 128), (128,))
-GIVE_AT = (None, (2, 3))
+MAINS = ((24, 48, 72, 95), (28, 57, 86, 115))
+GIVES = ((115, 128), (128,))
+GIVE_AT = (None, (2, 2))
 UNITS = 128
 
 
 def kernel(
     n, nf, mains, gives, give_at,
     t_hbm, q_hbm, c_hbm, count_ref, out_ref,
-    q_ref, gath, t_ref, c_ref, inv_ref, acc, part, red, t_tail, p_tail, tail_acc, tail_part,
+    q_ref, gath, t_ref, c_ref, inv_ref, acc, part, red, t_tail, p_tail, tail_acc, tail_part, tail_red,
     local_sem, recv_sem, share_sem, give_sem, ready_sem,
 ):
     me, f = lax.axis_index("loop"), lax.axis_index("feat")
     rows, width = t_ref.shape
     own_rows = rows // nf
+    queries = out_ref.shape[1]
+    tall = tail_part.shape[1]
+    fold = own_rows // tall
     q_rows = q_ref.shape[0]
     slots = max(len(cuts) for cuts in mains)
     has_left, has_right = me > 0, me < n - 1
@@ -83,19 +86,19 @@
         peer = lax.rem(f + k, nf)
         return pltpu.make_async_remote_copy(
             src_ref=tail_part.at[peer],
-            dst_ref=red.at[nf - 1 + k],
-            send_sem=local_sem.at[2],
-            recv_sem=share_sem.at[0],
+            dst_ref=tail_red.at[k],
+            send_sem=local_sem.at[3],
+            recv_sem=share_sem.at[1],
             device_id={"feat": peer, "loop": jnp.where(me == 1, 0, n - 1)},
             device_id_type=MESH,
         )
 
-    def all_shares(count):
+    def every(into, i):
         return pltpu.make_async_remote_copy(
-            src_ref=red.at[pl.ds(0, count)],
-            dst_ref=red.at[pl.ds(0, count)],
-            send_sem=local_sem.at[2],
-            recv_sem=share_sem.at[0],
+            src_ref=into,
+            dst_ref=into,
+            send_sem=local_sem.at[2 + i],
+            recv_sem=share_sem.at[i],
             device_id={"feat": lax.rem(f + 1, nf)},
             device_id_type=MESH,
         )
@@ -263,7 +266,10 @@
                     if i < len(gift) - 2:
                         tail_acc[...] = total
                 for k in range(nf):
-                    tail_part[k] = total[k * own_rows:(k + 1) * own_rows, :]
+                    tail_part[k] = jnp.concatenate(
+                        [total[a:a + tall, :] for a in range(k * own_rows, (k + 1) * own_rows, tall)],
+                        axis=1,
+                    )
                 for k in range(nf):
                     tail_share(k).start()
 
@@ -307,32 +313,33 @@
 
     live = f * own_rows + lax.broadcasted_iota(jnp.int32, out_ref.shape, 0) < count_ref[0]
 
-    def finish(count):
-        all_shares(count).wait_recv()
-        total = part[f]
-        for k in range(count):
-            total = total + red[k]
-        out_ref[...] = jnp.where(live, total, 0.0)
-
-    if mains[0][-1] == width:
-        finish(nf - 1)
-        all_shares(nf - 1).wait_send()
-    else:
+    if mains[0][-1] < width:
         @pl.when(is_end)
         def _():
-            finish(2 * nf - 1)
+            every(tail_red, 1).wait_recv()
+            more = tail_red[0]
+            for k in range(1, nf):
+                more = more + tail_red[k]
+            out_ref[...] = part[f] + jnp.concatenate(
+                [more[:, i * queries:(i + 1) * queries] for i in range(fold)], axis=0
+            )
 
         @pl.when(jnp.logical_not(is_end))
         def _():
-            finish(nf - 1)
-
+            out_ref[...] = part[f]
+    else:
+        out_ref[...] = part[f]
+
+    every(red, 0).wait_recv()
+    total = out_ref[...]
+    for k in range(nf - 1):
+        total = total + red[k]
+    out_ref[...] = jnp.where(live, total, 0.0)
+    every(red, 0).wait_send()
+    if mains[0][-1] < width:
         @pl.when(is_helper)
         def _():
-            all_shares(2 * nf - 1).wait_send()
-
-        @pl.when(jnp.logical_not(is_helper))
-        def _():
-            all_shares(nf - 1).wait_send()
+            every(tail_red, 1).wait_send()
 
 
 def on_device(n, nf, train_grads, query_grads, curvature, row_counts):
@@ -355,6 +362,8 @@
     tail = max(width - cuts[-1] for cuts in mains) or 128
     slots = max(len(cuts) for cuts in mains)
     lanes = -(-rows // 128) * 128
+    fold = max(1, min(128 // queries, rows // nf // 8))
+    folded = (nf, rows // nf // fold, queries * fold)
     hbm = pl.BlockSpec(memory_space=pltpu.HBM)
     return pl.pallas_call(
         functools.partial(kernel, n, nf, mains, gives, GIVE_AT),
@@ -369,14 +378,15 @@
             pltpu.VMEM((1, width), jnp.float32),
             pltpu.VMEM((queries, lanes), jnp.float32),
             pltpu.VMEM((nf, rows // nf, queries), jnp.float32),
-            pltpu.VMEM((2 * nf - 1, rows // nf, queries), jnp.float32),
+            pltpu.VMEM((nf - 1, rows // nf, queries), jnp.float32),
             pltpu.VMEM((rows, tail), jnp.bfloat16),
             pltpu.VMEM((queries, tail), jnp.float32),
             pltpu.VMEM((rows, queries), jnp.float32),
-            pltpu.VMEM((nf, rows // nf, queries), jnp.float32),
+            pltpu.VMEM(folded, jnp.float32),
+            pltpu.VMEM(folded, jnp.float32),
             pltpu.SemaphoreType.DMA((4,)),
             pltpu.SemaphoreType.DMA(((n - 1) * slots,)),
-            pltpu.SemaphoreType.DMA((1,)),
+            pltpu.SemaphoreType.DMA((2,)),
             pltpu.SemaphoreType.DMA((max(1, max(len(ends) - 1 for ends in gives)),)),
             pltpu.SemaphoreType.REGULAR,
         ],

time: 23.1 us -> 23 us (level)
  no operation moved by 1% of the time
where the time goes in v3:
time: 23 us; the launch traced here: 22.9 us
  Pallas kernels  21.6 us (94%)
  between operations  0.66 us (3%)
  local copies, waits for them, and re-layouts  0.6 us (3%)
    pallas_call x1, Pallas kernels, on_device(): pl.pallas_call(functools.partial(kernel, n, nf, mains, gives, GIVE_AT), o...  21.6 us
    unnamed x1, local copies, waits for them, and re-layouts  0.6 us

profile of v3, /device:TPU:0, one launch (start us, length us, event | category | flops | bytes accessed | tf_op | source)
XLA Modules:
  0.0 22.9 jit_solution(4638444891297826054)
XLA Ops:
  0.7 21.6 %shard_map.46 = f32[16,32]{1,0:T(8,128)S(1)} custom-call(bf16[64,16384]{1,0:T(8,128)(2,1)} %t_hbm.1, bf16[8,16384]{1,0:T(8,128)(2,1)} %q_hbm.1, f32[1,16384]{1,0:T(1,128)} %bitcast.1, s32[1]{0:T(128)S(6)} %copy.7.count_ref), custom_call_target="tpu_custom_call" | custom-call | tf_op jit(solution)/shard_map/pallas_call | solution.py:368
  22.3 0.6 %copy.6 = f32[16,32]{1,0:T(8,128)} copy(f32[16,32]{1,0:T(8,128)S(1)} %shard_map.46) | data formatting | bytes 4096

commit v4 on v3

--- a/solution.py
+++ b/solution.py
@@ -9,16 +9,15 @@
 
 MESH = pl.DeviceIdType.MESH
 damping_term = 0.1
-MAINS = ((24, 48, 72, 95), (28, 57, 86, 115))
-GIVES = ((115, 128), (128,))
+MAINS = ((24, 48, 72, 95), (29, 58, 87, 115))
 GIVE_AT = (None, (2, 2))
 UNITS = 128
 
 
 def kernel(
-    n, nf, mains, gives, give_at,
+    n, nf, mains, give_at,
     t_hbm, q_hbm, c_hbm, count_ref, out_ref,
-    q_ref, gath, t_ref, c_ref, inv_ref, acc, part, red, t_tail, p_tail, tail_acc, tail_part, tail_red,
+    q_ref, gath, t_ref, c_ref, inv_ref, acc, part, red, t_tail, p_tail, tail_part, tail_red,
     local_sem, recv_sem, share_sem, give_sem, ready_sem,
 ):
     me, f = lax.axis_index("loop"), lax.axis_index("feat")
@@ -103,7 +102,7 @@
             device_id_type=MESH,
         )
 
-    def run(cuts, gift, give_when):
+    def run(cuts, give_when):
         count = len(cuts) - 1
         main = cuts[-1]
         tail = main < width
@@ -136,20 +135,15 @@
                 for piece in pieces:
                     hop(way, me, piece, me + 2 * way - 1, own=True).start()
 
-        def give(i):
-            a, b = gift[i], gift[i + 1]
+        def give():
             return pltpu.make_async_remote_copy(
-                src_ref=t_ref.at[:, pl.ds(a, b - a)],
-                dst_ref=t_tail.at[:, pl.ds(a - main, b - a)],
+                src_ref=t_ref.at[:, pl.ds(main, width - main)],
+                dst_ref=t_tail.at[:, pl.ds(0, width - main)],
                 send_sem=local_sem.at[3],
-                recv_sem=give_sem.at[i],
+                recv_sem=give_sem.at[0],
                 device_id={"loop": jnp.where(is_first, 1, n - 2)},
                 device_id_type=MESH,
             )
-
-        def start_give():
-            for i in range(len(gift) - 1):
-                give(i).start()
 
         def multiply(block, piece, own=False):
             here = pl.ds(pl.multiple_of(block * q_rows, q_rows), q_rows)
@@ -210,7 +204,7 @@
         if tail and give_when is None:
             @pl.when(is_end)
             def _():
-                start_give()
+                give().start()
 
         inv_ref[...] = 1.0 / (damping_term + c_ref[...])
         for piece in range(count):
@@ -227,7 +221,7 @@
                 if tail and give_when is not None and piece == give_when[1]:
                     @pl.when(is_end & (back == n - give_when[0]))
                     def _():
-                        start_give()
+                        give().start()
 
             if tail:
                 for way in range(2):
@@ -249,22 +243,14 @@
         for k in range(1, nf):
             share(k).start()
 
-        def tail_dot(i):
-            at = pl.ds(gift[i] - main, gift[i + 1] - gift[i])
-            return lax.dot_general(
-                t_tail[:, at], p_tail[:, at].astype(jnp.bfloat16), (((1,), (1,)), ((), ())),
-                preferred_element_type=jnp.float32,
-            )
-
         if tail:
             @pl.when(is_helper)
             def _():
-                total = None
-                for i in range(len(gift) - 1):
-                    give(i).wait_recv()
-                    total = tail_dot(i) if total is None else tail_acc[...] + tail_dot(i)
-                    if i < len(gift) - 2:
-                        tail_acc[...] = total
+                give().wait_recv()
+                total = lax.dot_general(
+                    t_tail[:, 0:width - main], p_tail[:, 0:width - main].astype(jnp.bfloat16),
+                    (((1,), (1,)), ((), ())), preferred_element_type=jnp.float32,
+                )
                 for k in range(nf):
                     tail_part[k] = jnp.concatenate(
                         [total[a:a + tall, :] for a in range(k * own_rows, (k + 1) * own_rows, tall)],
@@ -293,23 +279,15 @@
         if tail:
             @pl.when(is_end)
             def _():
-                span = t_ref.at[:, pl.ds(main, width - main)]
-                pltpu.make_async_remote_copy(
-                    src_ref=span,
-                    dst_ref=span,
-                    send_sem=local_sem.at[3],
-                    recv_sem=give_sem.at[0],
-                    device_id={"loop": jnp.where(is_first, 1, n - 2)},
-                    device_id_type=MESH,
-                ).wait_send()
+                give().wait_send()
 
     if mains[0] == mains[1]:
-        run(mains[0], gives[0], give_at[0])
+        run(mains[0], give_at[0])
     else:
         for parity in range(2):
             @pl.when(lax.rem(f, 2) == parity)
             def _():
-                run(mains[parity], gives[parity], give_at[parity])
+                run(mains[parity], give_at[parity])
 
     live = f * own_rows + lax.broadcasted_iota(jnp.int32, out_ref.shape, 0) < count_ref[0]
 
@@ -352,13 +330,8 @@
 
     if n >= 4:
         mains = [[0] + [columns(cut) for cut in cuts] for cuts in MAINS]
-        gives = [
-            [cuts[-1]] + [columns(cut) for cut in ends[:-1]] + [width]
-            for cuts, ends in zip(mains, GIVES)
-        ]
     else:
         mains = [[0] + [columns(cut) for cut in (32, 64, 96)] + [width]] * 2
-        gives = [[width]] * 2
     tail = max(width - cuts[-1] for cuts in mains) or 128
     slots = max(len(cuts) for cuts in mains)
     lanes = -(-rows // 128) * 128
@@ -366,7 +339,7 @@
     folded = (nf, rows // nf // fold, queries * fold)
     hbm = pl.BlockSpec(memory_space=pltpu.HBM)
     return pl.pallas_call(
-        functools.partial(kernel, n, nf, mains, gives, GIVE_AT),
+        functools.partial(kernel, n, nf, mains, GIVE_AT),
         out_shape=pltpu.VMEM((rows // nf, queries), jnp.float32),
         in_specs=[hbm] * 3 + [pl.BlockSpec(memory_space=pltpu.SMEM)],
         out_specs=pl.BlockSpec(memory_space=pltpu.VMEM),
@@ -381,13 +354,12 @@
             pltpu.VMEM((nf - 1, rows // nf, queries), jnp.float32),
             pltpu.VMEM((rows, tail), jnp.bfloat16),
             pltpu.VMEM((queries, tail), jnp.float32),
-            pltpu.VMEM((rows, queries), jnp.float32),
             pltpu.VMEM(folded, jnp.float32),
             pltpu.VMEM(folded, jnp.float32),
             pltpu.SemaphoreType.DMA((4,)),
             pltpu.SemaphoreType.DMA(((n - 1) * slots,)),
             pltpu.SemaphoreType.DMA((2,)),
-            pltpu.SemaphoreType.DMA((max(1, max(len(ends) - 1 for ends in gives)),)),
+            pltpu.SemaphoreType.DMA((1,)),
             pltpu.SemaphoreType.REGULAR,
         ],
         compiler_params=pltpu.CompilerParams(collective_id=0, has_side_effects=True),

time: 23 us -> 23 us (level)
  no operation moved by 1% of the time
where the time goes in v4:
time: 23 us; the launch traced here: 22.8 us
  Pallas kernels  21.6 us (94%)
  between operations  0.66 us (3%)
  local copies, waits for them, and re-layouts  0.6 us (3%)
    pallas_call x1, Pallas kernels, on_device(): pl.pallas_call(functools.partial(kernel, n, nf, mains, GIVE_AT), out_shap...  21.6 us
    unnamed x1, local copies, waits for them, and re-layouts  0.6 us

profile of v4, /device:TPU:0, one launch (start us, length us, event | category | flops | bytes accessed | tf_op | source)
XLA Modules:
  0.0 22.8 jit_solution(5145708068818670938)
XLA Ops:
  0.7 21.6 %shard_map.46 = f32[16,32]{1,0:T(8,128)S(1)} custom-call(bf16[64,16384]{1,0:T(8,128)(2,1)} %t_hbm.1, bf16[8,16384]{1,0:T(8,128)(2,1)} %q_hbm.1, f32[1,16384]{1,0:T(1,128)} %bitcast.1, s32[1]{0:T(128)S(6)} %copy.7.count_ref), custom_call_target="tpu_custom_call" | custom-call | tf_op jit(solution)/shard_map/pallas_call | solution.py:341
  22.2 0.6 %copy.6 = f32[16,32]{1,0:T(8,128)} copy(f32[16,32]{1,0:T(8,128)S(1)} %shard_map.46) | data formatting | bytes 4096

commit v5 on v4

--- a/solution.py
+++ b/solution.py
@@ -240,7 +240,7 @@
         turned = acc[...].T
         for k in range(nf):
             part[k] = turned[k * own_rows:(k + 1) * own_rows, 0:part.shape[2]]
-        for k in range(1, nf):
+        for k in [*range(2, nf), 1]:
             share(k).start()
 
         if tail:

time: 23 us -> 23 us (level)
  no operation moved by 1% of the time
where the time goes in v5:
time: 23 us; the launch traced here: 22.8 us
  Pallas kernels  21.6 us (94%)
  between operations  0.66 us (3%)
  local copies, waits for them, and re-layouts  0.6 us (3%)
    pallas_call x1, Pallas kernels, on_device(): pl.pallas_call(functools.partial(kernel, n, nf, mains, GIVE_AT), out_shap...  21.6 us
    unnamed x1, local copies, waits for them, and re-layouts  0.6 us

profile of v5, /device:TPU:0, one launch (start us, length us, event | category | flops | bytes accessed | tf_op | source)
XLA Modules:
  0.0 22.8 jit_solution(11396214673769502635)
XLA Ops:
  0.7 21.6 %shard_map.46 = f32[16,32]{1,0:T(8,128)S(1)} custom-call(bf16[64,16384]{1,0:T(8,128)(2,1)} %t_hbm.1, bf16[8,16384]{1,0:T(8,128)(2,1)} %q_hbm.1, f32[1,16384]{1,0:T(1,128)} %bitcast.1, s32[1]{0:T(128)S(6)} %copy.7.count_ref), custom_call_target="tpu_custom_call" | custom-call | tf_op jit(solution)/shard_map/pallas_call | solution.py:341
  22.2 0.6 %copy.6 = f32[16,32]{1,0:T(8,128)} copy(f32[16,32]{1,0:T(8,128)S(1)} %shard_map.46) | data formatting | bytes 4096

commit v6 on v5

--- a/solution.py
+++ b/solution.py
@@ -9,7 +9,7 @@
 
 MESH = pl.DeviceIdType.MESH
 damping_term = 0.1
-MAINS = ((24, 48, 72, 95), (29, 58, 87, 115))
+MAINS = ((24, 48, 72, 94), (29, 58, 87, 116))
 GIVE_AT = (None, (2, 2))
 UNITS = 128
 

time: 23 us -> 23.1 us (level)
  no operation moved by 1% of the time
where the time goes in v6:
time: 23.1 us; the launch traced here: 23 us
  Pallas kernels  21.7 us (94%)
  between operations  0.66 us (3%)
  local copies, waits for them, and re-layouts  0.6 us (3%)
    pallas_call x1, Pallas kernels, on_device(): pl.pallas_call(functools.partial(kernel, n, nf, mains, GIVE_AT), out_shap...  21.7 us
    unnamed x1, local copies, waits for them, and re-layouts  0.6 us

profile of v6, /device:TPU:0, one launch (start us, length us, event | category | flops | bytes accessed | tf_op | source)
XLA Modules:
  0.0 23.0 jit_solution(13447013206550840312)
XLA Ops:
  0.7 21.7 %shard_map.46 = f32[16,32]{1,0:T(8,128)S(1)} custom-call(bf16[64,16384]{1,0:T(8,128)(2,1)} %t_hbm.1, bf16[8,16384]{1,0:T(8,128)(2,1)} %q_hbm.1, f32[1,16384]{1,0:T(1,128)} %bitcast.1, s32[1]{0:T(128)S(6)} %copy.7.count_ref), custom_call_target="tpu_custom_call" | custom-call | tf_op jit(solution)/shard_map/pallas_call | solution.py:341
  22.4 0.6 %copy.6 = f32[16,32]{1,0:T(8,128)} copy(f32[16,32]{1,0:T(8,128)S(1)} %shard_map.46) | data formatting | bytes 4096
